TPU v7x, 128 devices: a whole 4x4x4 slice. The times are simulated.
128 devices in a mesh: fsdp: 32 (over x_hi, z, y), tensor: 4 (over x_lo, core).
Axes of the slice: x: 4 (x_hi: 2, x_lo: 2; x = x_hi * 2 + x_lo), y: 4, z: 4, core: 2. Of those that a mesh axis runs over, the one named last changes fastest.
Arguments:
- activations: bfloat16 [32768, 5120], P('fsdp', 'tensor'), may hold values from -6 to 6
- cotangent: bfloat16 [32768, 5120], P('fsdp', 'tensor'), may hold values from -0.032958984 to 0.032958984
- weights: float32 [5120, 5120], P(None, ('tensor', 'fsdp')), may hold values from -0.025 to 0.025
- first_moment: float32 [5120, 5120], P(None, ('tensor', 'fsdp')), may hold values from -3 to 3
- second_moment: float32 [5120, 5120], P(None, ('tensor', 'fsdp')), may hold values from 0.01 to 1
Outputs:
- weights_new: float32 [5120, 5120], P('fsdp', 'tensor')
- first_new: float32 [5120, 5120], P('fsdp', 'tensor')
- second_new: float32 [5120, 5120], P('fsdp', 'tensor')
- weights_bf16: bfloat16 [5120, 5120], P(None, 'tensor')
All inputs are finite; a program needn't handle non-finite values.
Results may differ from a plain program's by a relative error of at most 0.014.
Values may be sent and summed in bfloat16 or wider, within the bound.
No kernel may reach another device: no remote copies, remote signals or barrier semaphores. Data moves between devices by JAX's collectives and lax.ppermute only.
A program may use at most 128 MiB of HBM per device.

v0:
```python
import jax
import jax.numpy as jnp
from jax import lax
from jax.sharding import PartitionSpec as P

STEP = 20
beta_one = 0.9
beta_two = 0.95
adam_eps = 1e-08
learn_rate = 0.0003
decay_rate = 0.1


def split_up(value, dim, count):
    before, after = (value.shape[:dim], value.shape[dim + 1 :])
    return jnp.moveaxis(value.reshape(*before, count, -1, *after), dim, 0)


def sent_and_summed(value, axis, dim):
    count = lax.axis_size(axis)
    parts = lax.all_to_all(split_up(value, dim, count), axis, 0, 0, tiled=True)
    return jnp.sum(parts.astype(jnp.float32), axis=0)


def adam_update(weights, first_moment, second_moment, gradient):
    first_new = beta_one * first_moment + (1.0 - beta_one) * gradient
    second_new = beta_two * second_moment + (1.0 - beta_two) * gradient * gradient
    corrected = first_new / (1.0 - beta_one**STEP)
    scaled = jnp.sqrt(second_new / (1.0 - beta_two**STEP)) + adam_eps
    weights_new = weights - learn_rate * (corrected / scaled + decay_rate * weights)
    return (weights_new, first_new, second_new)


def body(activations, cotangent, weights, first_moment, second_moment):
    gathered = lax.all_gather(activations, "tensor", axis=1, tiled=True)
    transposed = sent_and_summed(
        lax.dot_general(
            cotangent, gathered, (((0,), (0,)), ((), ())), preferred_element_type=jnp.float32
        ).astype(jnp.bfloat16),
        "fsdp",
        0,
    )
    gradient = transposed.T
    weights_old, first_old, second_old = adam_update(weights, first_moment, second_moment, gradient)
    weights_bf16 = lax.all_gather(weights_old.astype(jnp.bfloat16), "fsdp", axis=1, tiled=True)
    weights_new, first_new, second_new = (
        lax.all_to_all(
            weights_old.astype(jnp.bfloat16), "fsdp", split_axis=0, concat_axis=1, tiled=True
        ).astype(weights_old.dtype),
        lax.all_to_all(
            first_old.astype(jnp.bfloat16), "fsdp", split_axis=0, concat_axis=1, tiled=True
        ).astype(first_old.dtype),
        lax.all_to_all(
            second_old.astype(jnp.bfloat16), "fsdp", split_axis=0, concat_axis=1, tiled=True
        ).astype(second_old.dtype),
    )
    return (weights_new, first_new, second_new, weights_bf16)


def solution(mesh):
    return jax.shard_map(
        body,
        mesh=mesh,
        in_specs=(
            P("fsdp", "tensor"),
            P("fsdp", "tensor"),
            P(None, ("tensor", "fsdp")),
            P(None, ("tensor", "fsdp")),
            P(None, ("tensor", "fsdp")),
        ),
        out_specs=(
            P("fsdp", "tensor"),
            P("fsdp", "tensor"),
            P("fsdp", "tensor"),
            P(None, "tensor"),
        ),
        check_vma=False,
    )
```

profile of v0, /device:TPU:0, one launch (start us, length us, event | category | flops | bytes accessed | tf_op | source)
XLA Modules:
  0.0 469.7 jit_solution(9544911949169199346)
XLA Ops:
  7.2 0.0 copy-start
  7.2 0.0 all-gather.3.cloned.1.call-start
  7.2 0.7 all-gather.3.cloned.1.call-update
  7.9 0.0 all-gather.5.cloned.1.call-start
  8.0 101.3 %all-gather.3.cloned.1.call-done = bf16[1024,5120]{1,0:T(8,128)(2,1)} async-done(((bf16[1024,1280]{1,0:T(8,128)(2,1)}), bf16[1024,5120]{1,0:T(8,128)(2,1)}) %all-gather.3.cloned.1.call-update) | async-done | bytes 10485776 | tf_op jit(solution)/shard_map/all_gather | solution.py:35
  109.3 0.0 copy-done
  109.3 20.2 %convolution_convert_fusion = bf16[1280,5120]{1,0:T(8,128)(2,1)} fusion(bf16[1024,1280]{1,0:T(8,128)(2,1)S(1)} %copy-done, bf16[1024,5120]{1,0:T(8,128)(2,1)} %all-gather.3.cloned.1.call-done), kind=kOutput, calls=%fused_computation.1 | convolution fusion | flops 13428326400 | bytes 26214400 | tf_op jit(solution)/shard_map/dot_general | solution.py:37
  129.5 158.0 %all_to_all.44 = bf16[32,40,5120]{2,1,0:T(8,128)(2,1)} all-to-all(bf16[32,40,5120]{2,1,0:T(8,128)(2,1)} %bitcast.31), channel_id=1, replica_groups=mesh['fsdp'=32,'tensor'=4] {'fsdp'}, dimensions={0} | all-to-all | bytes 26214400 | tf_op jit(solution)/shard_map/all_to_all | solution.py:21
  287.4 0.0 copy-start.2
  287.4 0.0 copy-start.3
  287.4 7.7 %convert_reduce_fusion = f32[40,5120]{1,0:T(8,128)S(1)} fusion(bf16[32,40,5120]{2,1,0:T(8,128)(2,1)} %all_to_all.44), kind=kLoop, calls=%fused_computation | loop fusion | flops 12902400 | bytes 13926400 | tf_op jit(solution)/shard_map/reduce_sum | solution.py:22
  295.1 0.0 copy-done.2
  295.1 0.0 copy-done.3
  295.1 2.6 fusion.3
  297.7 0.0 all-gather.5.cloned.1.call-update
  297.7 0.8 all_to_all.38
  298.5 1.2 copy.28
  299.7 7.0 %all-to-all-start.3 = ((bf16[32,160,40]{1,2,0:T(8,128)(2,1)}), bf16[32,160,40]{1,2,0:T(8,128)(2,1)S(1)}, u32[]{:S(2)}, u32[]{:S(2)}) async-start(bf16[32,160,40]{1,2,0:T(8,128)(2,1)} %copy.28), calls=%async_computation.3 | async-start | bytes 1310720 | tf_op jit(solution)/shard_map/all_to_all | solution.py:53
  306.8 0.8 all_to_all.36
  307.6 1.2 copy.27
  308.8 13.6 %all-to-all-done.3 = bf16[32,160,40]{1,2,0:T(8,128)(2,1)S(1)} async-done(((bf16[32,160,40]{1,2,0:T(8,128)(2,1)}), bf16[32,160,40]{1,2,0:T(8,128)(2,1)S(1)}, u32[]{:S(2)}, u32[]{:S(2)}) %all-to-all-start.3) | async-done | bytes 409632 | tf_op jit(solution)/shard_map/all_to_all | solution.py:53
  322.4 4.7 %all-to-all-start.2 = ((bf16[32,160,40]{1,2,0:T(8,128)(2,1)}), bf16[32,160,40]{1,2,0:T(8,128)(2,1)S(1)}, u32[]{:S(2)}, u32[]{:S(2)}) async-start(bf16[32,160,40]{1,2,0:T(8,128)(2,1)} %copy.27), calls=%async_computation.2 | async-start | bytes 1310720 | tf_op jit(solution)/shard_map/all_to_all | solution.py:50
  327.1 1.8 all_to_all.34
  328.9 1.2 copy.26
  330.1 10.4 %all-to-all-done.2 = bf16[32,160,40]{1,2,0:T(8,128)(2,1)S(1)} async-done(((bf16[32,160,40]{1,2,0:T(8,128)(2,1)}), bf16[32,160,40]{1,2,0:T(8,128)(2,1)S(1)}, u32[]{:S(2)}, u32[]{:S(2)}) %all-to-all-start.2) | async-done | bytes 409632 | tf_op jit(solution)/shard_map/all_to_all | solution.py:50
  340.5 4.0 all-to-all-start.1
  344.5 0.1 convert_element_type.62
  344.6 1.3 copy.31
  345.9 0.1 convert_element_type.61
  346.0 1.3 copy.30
  347.2 16.4 %all-to-all-done.1 = bf16[32,160,40]{1,2,0:T(8,128)(2,1)S(1)} async-done(((bf16[32,160,40]{1,2,0:T(8,128)(2,1)}), bf16[32,160,40]{1,2,0:T(8,128)(2,1)S(1)}, u32[]{:S(2)}, u32[]{:S(2)}) %all-to-all-start.1) | async-done | bytes 409632 | tf_op jit(solution)/shard_map/all_to_all | solution.py:47
  363.6 1.2 convert_element_type.60
  364.8 0.0 copy-start.1
  364.8 2.7 copy.29
  367.5 77.8 %all-gather.5.cloned.1.call-done = bf16[5120,1280]{0,1:T(8,128)(2,1)} async-done(((bf16[5120,40]{0,1:T(8,128)(2,1)}), bf16[5120,1280]{0,1:T(8,128)(2,1)}) %all-gather.5.cloned.1.call-update) | async-done | bytes 13107216 | tf_op jit(solution)/shard_map/all_gather | solution.py:45
  445.3 17.6 %copy.32 = bf16[5120,1280]{1,0:T(8,128)(2,1)} copy(bf16[5120,1280]{0,1:T(8,128)(2,1)} %all-gather.5.cloned.1.call-done) | data formatting | bytes 26214400
  462.8 0.0 copy-done.1
Async XLA Ops:
  7.2 102.1 %copy-start = (bf16[1024,1280]{1,0:T(8,128)(2,1)S(1)}, bf16[1024,1280]{1,0:T(8,128)(2,1)}, u32[]{:S(2)}) copy-start(bf16[1024,1280]{1,0:T(8,128)(2,1)} %param.6) | copy-start | bytes 7864324
  7.2 102.1 %all-gather.3.cloned.1.call-start = ((), (), s32[]{:S(2)}) async-start(), calls=%async_computation.4 | async-start | bytes 13107200 | tf_op jit(solution)/shard_map/all_gather | solution.py:35
  7.9 437.4 %all-gather.5.cloned.1.call-start = ((), (), s32[]{:S(2)}) async-start(), calls=%async_computation.5 | async-start | bytes 13516800 | tf_op jit(solution)/shard_map/all_gather | solution.py:45
  287.4 7.7 %copy-start.2 = (f32[5120,40]{0,1:T(8,128)S(1)}, f32[5120,40]{0,1:T(8,128)}, u32[]{:S(2)}) copy-start(f32[5120,40]{0,1:T(8,128)} %param.9) | copy-start | bytes 2457604
  287.4 7.7 %copy-start.3 = (f32[5120,40]{0,1:T(8,128)S(1)}, f32[5120,40]{0,1:T(8,128)}, u32[]{:S(2)}) copy-start(f32[5120,40]{0,1:T(8,128)} %param.7) | copy-start | bytes 2457604
  299.7 22.6 %all-to-all-start.3 = ((bf16[32,160,40]{1,2,0:T(8,128)(2,1)}), bf16[32,160,40]{1,2,0:T(8,128)(2,1)S(1)}, u32[]{:S(2)}, u32[]{:S(2)}) async-start(bf16[32,160,40]{1,2,0:T(8,128)(2,1)} %copy.28), calls=%async_computation.3 | async-start | bytes 1310720 | tf_op jit(solution)/shard_map/all_to_all | solution.py:53
  322.4 18.1 %all-to-all-start.2 = ((bf16[32,160,40]{1,2,0:T(8,128)(2,1)}), bf16[32,160,40]{1,2,0:T(8,128)(2,1)S(1)}, u32[]{:S(2)}, u32[]{:S(2)}) async-start(bf16[32,160,40]{1,2,0:T(8,128)(2,1)} %copy.27), calls=%async_computation.2 | async-start | bytes 1310720 | tf_op jit(solution)/shard_map/all_to_all | solution.py:50
  340.5 23.1 %all-to-all-start.1 = ((bf16[32,160,40]{1,2,0:T(8,128)(2,1)}), bf16[32,160,40]{1,2,0:T(8,128)(2,1)S(1)}, u32[]{:S(2)}, u32[]{:S(2)}) async-start(bf16[32,160,40]{1,2,0:T(8,128)(2,1)} %copy.26), calls=%async_computation.1 | async-start | bytes 1310720 | tf_op jit(solution)/shard_map/all_to_all | solution.py:47
  364.8 98.1 %copy-start.1 = (bf16[1024,1280]{1,0:T(8,128)(2,1)S(1)}, bf16[1024,1280]{1,0:T(8,128)(2,1)}, u32[]{:S(2)}) copy-start(bf16[1024,1280]{1,0:T(8,128)(2,1)} %param.6) | copy-start | bytes 7864324
Sparse Core Ops, SparseCore 0:
  9.6 99.5 all-gather.2
  297.8 147.3 all-gather.4
where the time goes:
time: 471 us; the launch traced here: 470 us
  waiting for transfers between devices  220 us (47%)
  blocking collectives  158 us (34%)
  local copies, waits for them, and re-layouts  29.9 us (6%)
  matrix products  20.2 us (4%)
  starting transfers between devices  15.8 us (3%)
  between operations  14.1 us (3%)
  other arithmetic  11.6 us (2%)
    all_to_all x1, blocking collectives, sent_and_summed(): parts = lax.all_to_all(split_up(value, dim, count), axis, 0, 0, tiled=True)  158 us
    all_gather x1, waiting for transfers between devices, body(): gathered = lax.all_gather(activations, 'tensor', axis=1, tiled=True)  101 us
    all_gather x1, waiting for transfers between devices, body(): lax.all_gather(weights_old.astype(jnp.bfloat16), 'fsdp', axis=1, tiled=True)  77.8 us
    unnamed x12, local copies, waits for them, and re-layouts  22.9 us
    dot_general x1, matrix products, body(): lax.dot_general(cotangent, gathered, (((0,), (0,)), ((), ())), preferred_...  20.2 us
    all_to_all x1, waiting for transfers between devices, body(): lax.all_to_all(weights_old.astype(jnp.bfloat16), 'fsdp', split_axis=0, co...  16.4 us
    all_to_all x1, waiting for transfers between devices, body(): lax.all_to_all(second_old.astype(jnp.bfloat16), 'fsdp', split_axis=0, con...  13.6 us
    all_to_all x1, waiting for transfers between devices, body(): lax.all_to_all(first_old.astype(jnp.bfloat16), 'fsdp', split_axis=0, conc...  10.4 us
  transfers between devices with their start and end apart: 5, of which 5 were waited for; matrix products, arithmetic and copies ran while one was open for 2% of the time, Pallas kernels for 0%

commit v1 on v0

--- a/solution.py
+++ b/solution.py
@@ -42,7 +42,12 @@
     )
     gradient = transposed.T
     weights_old, first_old, second_old = adam_update(weights, first_moment, second_moment, gradient)
-    weights_bf16 = lax.all_gather(weights_old.astype(jnp.bfloat16), "fsdp", axis=1, tiled=True)
+    weights_bf16 = jnp.concatenate(
+        lax.all_to_all(
+            jnp.stack([weights_old.astype(jnp.bfloat16)] * lax.axis_size("fsdp")), "fsdp", 0, 0
+        ),
+        axis=1,
+    )
     weights_new, first_new, second_new = (
         lax.all_to_all(
             weights_old.astype(jnp.bfloat16), "fsdp", split_axis=0, concat_axis=1, tiled=True

time: 471 us -> 603 us (1.28)
  the two profiles are of different devices: /device:TPU:0 before, /device:TPU:98 now
where the time goes in v1:
time: 603 us; the launch traced here: 602 us
  waiting for transfers between devices  323 us (54%)
  blocking collectives  176 us (29%)
  local copies, waits for them, and re-layouts  34.3 us (6%)
  starting transfers between devices  22.4 us (4%)
  matrix products  20.2 us (3%)
  between operations  14.1 us (2%)
  other arithmetic  11.6 us (2%)
    all_to_all x1, waiting for transfers between devices, body(): lax.all_to_all(jnp.stack([weights_old.astype(jnp.bfloat16)] * lax.axis_si...  200 us
    all_to_all x1, blocking collectives, sent_and_summed(): parts = lax.all_to_all(split_up(value, dim, count), axis, 0, 0, tiled=True)  158 us
    all_gather x1, waiting for transfers between devices, body(): gathered = lax.all_gather(activations, 'tensor', axis=1, tiled=True)  100 us
    unnamed x12, local copies, waits for them, and re-layouts  21.5 us
    dot_general x1, matrix products, body(): lax.dot_general(cotangent, gathered, (((0,), (0,)), ((), ())), preferred_...  20.2 us
    all_to_all x1, blocking collectives, body(): lax.all_to_all(second_old.astype(jnp.bfloat16), 'fsdp', split_axis=0, con...  17.4 us
  transfers between devices with their start and end apart: 4, of which 4 were waited for; matrix products, arithmetic and copies ran while one was open for 1% of the time, Pallas kernels for 0%

profile of v1, /device:TPU:98, one launch (start us, length us, event | category | flops | bytes accessed | tf_op | source)
XLA Modules:
  0.0 601.8 jit_solution(14103812240310579471)
XLA Ops:
  7.2 0.0 copy-start
  7.2 0.0 all-gather.2.cloned.1.call-start
  7.2 0.7 all-gather.2.cloned.1.call-update
  7.9 100.1 %all-gather.2.cloned.1.call-done = bf16[1024,5120]{1,0:T(8,128)(2,1)} async-done(((bf16[1024,1280]{1,0:T(8,128)(2,1)}), bf16[1024,5120]{1,0:T(8,128)(2,1)}) %all-gather.2.cloned.1.call-update) | async-done | bytes 10485776 | tf_op jit(solution)/shard_map/all_gather | solution.py:35
  108.0 0.0 copy-done
  108.0 20.2 %convolution_convert_fusion = bf16[1280,5120]{1,0:T(8,128)(2,1)} fusion(bf16[1024,1280]{1,0:T(8,128)(2,1)S(1)} %copy-done, bf16[1024,5120]{1,0:T(8,128)(2,1)} %all-gather.2.cloned.1.call-done), kind=kOutput, calls=%fused_computation.1 | convolution fusion | flops 13428326400 | bytes 26214400 | tf_op jit(solution)/shard_map/dot_general | solution.py:37
  128.2 158.4 %all_to_all.49 = bf16[32,40,5120]{2,1,0:T(8,128)(2,1)} all-to-all(bf16[32,40,5120]{2,1,0:T(8,128)(2,1)} %bitcast.34), channel_id=1, replica_groups=mesh['fsdp'=32,'tensor'=4] {'fsdp'}, dimensions={0} | all-to-all | bytes 26214400 | tf_op jit(solution)/shard_map/all_to_all | solution.py:21
  286.7 0.0 copy-start.2
  286.7 0.0 copy-start.3
  286.7 7.7 %convert_reduce_fusion = f32[40,5120]{1,0:T(8,128)S(1)} fusion(bf16[32,40,5120]{2,1,0:T(8,128)(2,1)} %all_to_all.49), kind=kLoop, calls=%fused_computation | loop fusion | flops 12902400 | bytes 13926400 | tf_op jit(solution)/shard_map/reduce_sum | solution.py:22
  294.3 0.0 copy-done.2
  294.3 0.0 copy-done.3
  294.4 2.5 fusion.3
  296.9 0.8 all_to_all.37
  297.7 1.2 copy.13
  298.9 11.0 %all-to-all-start.1 = ((bf16[32,160,40]{1,2,0:T(8,128)(2,1)}), bf16[32,160,40]{1,2,0:T(8,128)(2,1)S(1)}, u32[]{:S(2)}, u32[]{:S(2)}) async-start(bf16[32,160,40]{1,2,0:T(8,128)(2,1)} %copy.13), calls=%async_computation.1 | async-start | bytes 1310720 | tf_op jit(solution)/shard_map/all_to_all | solution.py:52
  309.9 0.8 all_to_all.39
  310.8 1.2 copy.14
  312.0 11.5 %all-to-all-done.1 = bf16[32,160,40]{1,2,0:T(8,128)(2,1)S(1)} async-done(((bf16[32,160,40]{1,2,0:T(8,128)(2,1)}), bf16[32,160,40]{1,2,0:T(8,128)(2,1)S(1)}, u32[]{:S(2)}, u32[]{:S(2)}) %all-to-all-start.1) | async-done | bytes 409632 | tf_op jit(solution)/shard_map/all_to_all | solution.py:52
  323.5 5.3 all-to-all-start.2
  328.8 1.8 all_to_all.41
  330.6 0.4 copy.15
  331.0 10.8 %all-to-all-done.2 = bf16[32,160,40]{1,2,0:T(8,128)(2,1)S(1)} async-done(((bf16[32,160,40]{1,2,0:T(8,128)(2,1)}), bf16[32,160,40]{1,2,0:T(8,128)(2,1)S(1)}, u32[]{:S(2)}, u32[]{:S(2)}) %all-to-all-start.2) | async-done | bytes 409632 | tf_op jit(solution)/shard_map/all_to_all | solution.py:55
  341.8 17.4 %all_to_all.50 = bf16[32,160,40]{1,2,0:T(8,128)(2,1)} all-to-all(bf16[32,160,40]{1,2,0:T(8,128)(2,1)S(1)} %copy.15), channel_id=1, replica_groups=mesh['fsdp'=32,'tensor'=4] {'fsdp'}, dimensions={0} | all-to-all | bytes 819200 | tf_op jit(solution)/shard_map/all_to_all | solution.py:58
  359.2 6.6 %stack.2 = bf16[32,5120,40]{1,2,0:T(8,128)(2,1)} broadcast(bf16[5120,40]{0,1:T(8,128)(2,1)S(1)} %get-tuple-element.9), dimensions={1,2} | broadcast | bytes 13516800 | tf_op jit(solution)/shard_map/stack | solution.py:47
  365.8 6.1 %all-to-all-start.4 = ((bf16[32,5120,40]{1,2,0:T(8,128)(2,1)}), bf16[32,5120,40]{1,2,0:T(8,128)(2,1)}, u32[]{:S(2)}, u32[]{:S(2)}) async-start(bf16[32,5120,40]{1,2,0:T(8,128)(2,1)} %stack.2), calls=%async_computation.4 | async-start | bytes 26214400 | tf_op jit(solution)/shard_map/all_to_all | solution.py:46
  371.9 0.1 convert_element_type.60
  372.0 1.3 copy.16
  373.3 0.1 convert_element_type.61
  373.4 1.3 copy.17
  374.6 1.2 convert_element_type.62
  375.8 1.3 copy.18
  377.1 200.1 %all-to-all-done.4 = bf16[32,5120,40]{1,2,0:T(8,128)(2,1)} async-done(((bf16[32,5120,40]{1,2,0:T(8,128)(2,1)}), bf16[32,5120,40]{1,2,0:T(8,128)(2,1)}, u32[]{:S(2)}, u32[]{:S(2)}) %all-to-all-start.4) | async-done | bytes 13107232 | tf_op jit(solution)/shard_map/all_to_all | solution.py:46
  577.2 0.0 copy-start.1
  577.2 17.7 %copy.19 = bf16[5120,1280]{1,0:T(8,128)(2,1)} copy(bf16[5120,1280]{0,1:T(8,128)(2,1)} %bitcast.9) | data formatting | bytes 26214400
  594.9 0.0 copy-done.1
Async XLA Ops:
  7.2 100.9 %copy-start = (bf16[1024,1280]{1,0:T(8,128)(2,1)S(1)}, bf16[1024,1280]{1,0:T(8,128)(2,1)}, u32[]{:S(2)}) copy-start(bf16[1024,1280]{1,0:T(8,128)(2,1)} %param.6) | copy-start | bytes 7864324
  7.2 100.9 %all-gather.2.cloned.1.call-start = ((), (), s32[]{:S(2)}) async-start(), calls=%async_computation.5 | async-start | bytes 13107200 | tf_op jit(solution)/shard_map/all_gather | solution.py:35
  286.7 7.7 %copy-start.2 = (f32[5120,40]{0,1:T(8,128)S(1)}, f32[5120,40]{0,1:T(8,128)}, u32[]{:S(2)}) copy-start(f32[5120,40]{0,1:T(8,128)} %param.9) | copy-start | bytes 2457604
  286.7 7.7 %copy-start.3 = (f32[5120,40]{0,1:T(8,128)S(1)}, f32[5120,40]{0,1:T(8,128)}, u32[]{:S(2)}) copy-start(f32[5120,40]{0,1:T(8,128)} %param.7) | copy-start | bytes 2457604
  298.9 24.6 %all-to-all-start.1 = ((bf16[32,160,40]{1,2,0:T(8,128)(2,1)}), bf16[32,160,40]{1,2,0:T(8,128)(2,1)S(1)}, u32[]{:S(2)}, u32[]{:S(2)}) async-start(bf16[32,160,40]{1,2,0:T(8,128)(2,1)} %copy.13), calls=%async_computation.1 | async-start | bytes 1310720 | tf_op jit(solution)/shard_map/all_to_all | solution.py:52
  323.5 18.3 %all-to-all-start.2 = ((bf16[32,160,40]{1,2,0:T(8,128)(2,1)}), bf16[32,160,40]{1,2,0:T(8,128)(2,1)S(1)}, u32[]{:S(2)}, u32[]{:S(2)}) async-start(bf16[32,160,40]{1,2,0:T(8,128)(2,1)} %copy.14), calls=%async_computation.2 | async-start | bytes 1310720 | tf_op jit(solution)/shard_map/all_to_all | solution.py:55
  365.8 211.4 %all-to-all-start.4 = ((bf16[32,5120,40]{1,2,0:T(8,128)(2,1)}), bf16[32,5120,40]{1,2,0:T(8,128)(2,1)}, u32[]{:S(2)}, u32[]{:S(2)}) async-start(bf16[32,5120,40]{1,2,0:T(8,128)(2,1)} %stack.2), calls=%async_computation.4 | async-start | bytes 26214400 | tf_op jit(solution)/shard_map/all_to_all | solution.py:46
  577.2 17.7 %copy-start.1 = (bf16[1024,1280]{1,0:T(8,128)(2,1)S(1)}, bf16[1024,1280]{1,0:T(8,128)(2,1)}, u32[]{:S(2)}) copy-start(bf16[1024,1280]{1,0:T(8,128)(2,1)} %param.6) | copy-start | bytes 7864324
Sparse Core Ops, SparseCore 0:
  9.6 98.3 all-gather.1
